TPU v7x, 32 devices: a whole 2x2x4 slice. The times are simulated.
32 devices in a mesh: groups: 2 (over y), ep: 4 (over x, core), tp: 4 (over z).
Axes of the slice: x: 2, y: 2, z: 4, core: 2. Of those that a mesh axis runs over, the one named last changes fastest.
Arguments:
- hidden_in: bfloat16 [32, 4, 3584], P(('groups', 'ep', 'tp')), parts along dimension 0, may hold values from -12 to 12
- queries: bfloat16 [32, 4, 128, 576], P(('groups', 'ep', 'tp')), parts along dimension 0, may hold values from -100 to 100
- kv_cache: bfloat16 [32, 2048, 576], P(('groups', 'ep', 'tp')), parts along dimension 0, may hold values from -6 to 6
- new_kv: bfloat16 [32, 4, 576], P(('groups', 'ep', 'tp')), parts along dimension 0, may hold values from -8 to 8
- lengths: int32 [32], P(('groups', 'ep', 'tp')), parts along dimension 0, may hold values from 128 to 2048, as said below
- expert_ids: int32 [32, 4, 2], P(('groups', 'ep')), parts along dimension 0, may hold values from 0 to 3, all different within a row; in each aligned block of 16 rows (0 to 15, 16 to 31, ..., all dimensions but the last counted through in order) at most 12 rows name the same one
- value_up: bfloat16 [128, 512, 128], P(('ep', 'tp')), may hold values from -3 to 3
- out_proj: bfloat16 [128, 128, 3584], P(('ep', 'tp')), may hold values from -0.046875 to 0.046875
- norm_gain: bfloat16 [3584], replicated, may hold values from 0.099609375 to 1.8984375
- router: bfloat16 [3584, 4], replicated, may hold values from -0.09375 to 0.09375
- expert_in: bfloat16 [4, 2, 3584, 2048], P('ep', None, None, 'tp'), may hold values from -0.09375 to 0.09375
- expert_out: bfloat16 [4, 2048, 3584], P('ep', 'tp'), may hold values from -0.125 to 0.125
- shared_in: bfloat16 [2, 3584, 1024], P(None, None, 'tp'), may hold values from -0.09375 to 0.09375
- shared_out: bfloat16 [1024, 3584], P('tp'), may hold values from -0.1875 to 0.1875
Outputs:
- layer_out: bfloat16 [32, 4, 3584], P(('groups', 'ep', 'tp')), parts along dimension 0
There are 2 independent parts, one for each index of `groups`. A program takes and returns all parts, laid end to end along the dimension named above; an argument that names none is the same for every part. Nothing has to cross between parts.
Inputs may be any that keep to these rules, and one draw needn't show every extreme that they name: `expert_ids`: each row and step names 2 distinct experts; within the rows of one index of ep, over all 4 steps, no expert is named more than 12 times, and in every draw some expert is named exactly 12 times there. `lengths`: some row uses all 2048 cached positions.
All inputs are finite; a program needn't handle non-finite values.
Results may differ from a plain program's by a relative error of at most 0.014.
Values may be sent and summed in bfloat16 or wider, within the bound.
No kernel may reach another device: no remote copies, remote signals or barrier semaphores. Data moves between devices by JAX's collectives and lax.ppermute only.
A program may use at most 64 MiB of HBM per device.

v0:
```python
import jax
import jax.numpy as jnp
from jax import lax
from jax.sharding import PartitionSpec as P

LAT = 512
score_scale = 192.0 ** (-0.5)
route_scale = 2.5
norm_eps = 1e-06


def attend_block(queries, kv_cache, new_kv, lengths):
    rows_here, steps_here, heads_here, kv_width = queries.shape
    positions = kv_cache.shape[1]
    cached = (
        jnp.einsum("rshk,rck->rshc", queries, kv_cache, preferred_element_type=jnp.float32)
        * score_scale
    )
    recent = (
        jnp.einsum("rshk,rjk->rshj", queries, new_kv, preferred_element_type=jnp.float32)
        * score_scale
    )
    cache_live = lax.broadcasted_iota(jnp.int32, (rows_here, positions), 1) < lengths[:, None]
    causal = lax.broadcasted_iota(jnp.int32, (steps_here, steps_here), 1) <= lax.broadcasted_iota(
        jnp.int32, (steps_here, steps_here), 0
    )
    cached = jnp.where(cache_live[:, None, None, :], cached, -1e30)
    recent = jnp.where(causal[None, :, None, :], recent, -1e30)
    highest = jnp.maximum(cached.max(-1), recent.max(-1))[..., None]
    cached_exp = jnp.exp(cached - highest)
    recent_exp = jnp.exp(recent - highest)
    denominator = cached_exp.sum(-1, keepdims=True) + recent_exp.sum(-1, keepdims=True)
    cached_prob = (cached_exp / denominator).astype(jnp.bfloat16)
    recent_prob = (recent_exp / denominator).astype(jnp.bfloat16)
    combined = jnp.einsum(
        "rshc,rck->rshk", cached_prob, kv_cache, preferred_element_type=jnp.float32
    )
    combined = combined + jnp.einsum(
        "rshj,rjk->rshk", recent_prob, new_kv, preferred_element_type=jnp.float32
    )
    return combined[..., :LAT].astype(jnp.bfloat16)


def on_device(
    hidden_in,
    queries,
    kv_cache,
    new_kv,
    lengths,
    expert_ids,
    value_up,
    out_proj,
    norm_gain,
    router,
    expert_in,
    expert_out,
    shared_in,
    shared_out,
):
    rows_here = hidden_in.shape[0]
    steps_here = hidden_in.shape[1]
    model_width = hidden_in.shape[2]
    latent_out = attend_block(queries, kv_cache, new_kv, lengths)
    by_head = lax.all_to_all(latent_out, ("ep", "tp"), split_axis=2, concat_axis=0, tiled=True)
    head_vals = jnp.einsum(
        "rshl,hlv->rshv", by_head, value_up, preferred_element_type=jnp.float32
    ).astype(jnp.bfloat16)
    attention = lax.psum_scatter(
        jnp.einsum("rshv,hvd->rsd", head_vals, out_proj, preferred_element_type=jnp.float32),
        ("ep", "tp"),
        scatter_dimension=0,
        tiled=True,
    )
    residual = hidden_in.astype(jnp.float32) + attention
    mean_square = jnp.mean(residual * residual, axis=-1, keepdims=True)
    normed = (residual * lax.rsqrt(mean_square + norm_eps) * norm_gain.astype(jnp.float32)).astype(
        jnp.bfloat16
    )
    block_items = lax.all_gather(
        normed.reshape(rows_here * steps_here, model_width), "tp", axis=0, tiled=True
    )
    item_count = block_items.shape[0]
    expert_count = router.shape[1]
    capacity = 3 * item_count // 4
    affinity = jax.nn.sigmoid(jnp.dot(block_items, router, preferred_element_type=jnp.float32))
    picked = expert_ids.reshape(item_count, expert_ids.shape[2])
    expert_iota = lax.broadcasted_iota(jnp.int32, (1, 1, expert_count), 2)
    chosen = jnp.sum((picked[:, :, None] == expert_iota).astype(jnp.int32), axis=1)
    scored = chosen.astype(jnp.float32) * affinity
    gate_weight = route_scale * scored / jnp.sum(scored, axis=-1, keepdims=True)
    slot_index = jnp.cumsum(chosen, axis=0) - chosen
    slot_iota = lax.broadcasted_iota(jnp.int32, (1, 1, capacity), 2)
    slot_hit = (slot_index[:, :, None] == slot_iota) & (chosen[:, :, None] > 0)
    outgoing = jnp.einsum(
        "mux,mt->uxt",
        slot_hit.astype(jnp.bfloat16),
        block_items,
        preferred_element_type=jnp.float32,
    ).astype(jnp.bfloat16)
    arrived = lax.all_to_all(outgoing, "ep", split_axis=0, concat_axis=0, tiled=True)
    gate_part = jnp.einsum(
        "scd,df->scf", arrived, expert_in[0, 0], preferred_element_type=jnp.float32
    )
    up_part = jnp.einsum(
        "scd,df->scf", arrived, expert_in[0, 1], preferred_element_type=jnp.float32
    )
    activated = (jax.nn.silu(gate_part) * up_part).astype(jnp.bfloat16)
    produced = jnp.einsum(
        "scf,fd->scd", activated, expert_out[0], preferred_element_type=jnp.float32
    )
    returned_slots = lax.all_to_all(
        produced.astype(jnp.bfloat16), "ep", split_axis=0, concat_axis=0, tiled=True
    ).astype(produced.dtype)
    combine = jnp.where(slot_hit, gate_weight[:, :, None], 0.0)
    routed_part = jnp.einsum(
        "jpo,pos->js",
        combine,
        returned_slots,
        precision=lax.Precision.HIGHEST,
        preferred_element_type=jnp.float32,
    )
    shared_gate = jnp.dot(block_items, shared_in[0], preferred_element_type=jnp.float32)
    shared_up = jnp.dot(block_items, shared_in[1], preferred_element_type=jnp.float32)
    shared_act = (jax.nn.silu(shared_gate) * shared_up).astype(jnp.bfloat16)
    shared_part = jnp.dot(shared_act, shared_out, preferred_element_type=jnp.float32)
    expert_sum = lax.psum_scatter(
        (routed_part + shared_part).astype(jnp.bfloat16), "tp", scatter_dimension=0, tiled=True
    ).astype(jnp.float32)
    layer_out = (residual + expert_sum.reshape(rows_here, steps_here, model_width)).astype(
        jnp.bfloat16
    )
    return layer_out


def solution(mesh):
    in_specs = (
        P(("groups", "ep", "tp"), None, None),
        P(("groups", "ep", "tp"), None, None, None),
        P(("groups", "ep", "tp"), None, None),
        P(("groups", "ep", "tp"), None, None),
        P(("groups", "ep", "tp")),
        P(("groups", "ep"), None, None),
        P(("ep", "tp"), None, None),
        P(("ep", "tp"), None, None),
        P(),
        P(),
        P("ep", None, None, "tp"),
        P("ep", "tp", None),
        P(None, None, "tp"),
        P("tp", None),
    )
    out_specs = P(("groups", "ep", "tp"), None, None)
    return jax.shard_map(
        on_device, mesh=mesh, in_specs=in_specs, out_specs=out_specs, check_vma=False
    )
```

profile of v0, /device:TPU:0, one launch (start us, length us, event | category | flops | bytes accessed | tf_op | source)
XLA Modules:
  0.0 234.1 jit_solution(7596553311977979096)
XLA Ops:
  7.4 0.8 copy-done
  8.2 3.2 %fusion.6 = (f32[4,128]{1,0:T(4,128)S(1)}, f32[4,128,2048]{2,1,0:T(8,128)S(1)}) fusion(pred[2048]{0:T(1024)(128)(4,1)S(1)} %iota_compare_fusion.1, bf16[1,2048,576]{1,2,0:T(8,128)(2,1)S(1)} %copy-done, bf16[1,4,128,576]{2,3,1,0:T(8,128)(2,1)} %param.15), kind=kOutput, calls=%fused_computation.11 | convolution fusion | flops 1211104768 | bytes 7147520 | tf_op jit(solution)/shard_map/rshk,rck->rshc/dot_general | solution.py:16
  11.6 0.9 fusion.14
  12.6 1.7 fusion.15
  15.1 22.8 %all_to_all.28 = bf16[1,4,128,512]{3,1,0,2:T(4,128)(2,1)} all-to-all(bf16[1,4,128,512]{3,1,0,2:T(4,128)(2,1)S(1)} %copy.40), channel_id=1, replica_groups=mesh['groups'=2,'ep'=4,'tp'=4] {'ep','tp'}, dimensions={2} | all-to-all | bytes 1048576 | tf_op jit(solution)/shard_map/all_to_all | solution.py:64
  38.0 5.3 %fusion.2 = f32[16,4,3584]{2,0,1:T(8,128)S(1)} fusion(bf16[8,128,3584]{2,1,0:T(8,128)(2,1)} %param.21, bf16[8,512,128]{2,1,0:T(8,128)(2,1)} %param.20, bf16[1,4,16,8,512]{4,1,3,2,0:T(4,128)(2,1)} %bitcast.112), kind=kOutput, calls=%fused_computation.2 | convolution fusion | flops 536936448 | bytes 9830400 | tf_op jit(solution)/shard_map/rshv,hvd->rsd/dot_general | solution.py:69
  43.3 1.6 copy.43
  45.3 0.6 dynamic-slice
  45.9 90.4 %all-reduce.5.cloned.1.call-done = f32[16,4,3584]{2,1,0:T(4,128)} async-done(((f32[16,4,3584]{2,1,0:T(4,128)}), f32[16,4,3584]{2,1,0:T(4,128)}) %all-reduce.5.cloned.1.call-update) | async-done | bytes 917520
  136.2 1.5 multiply_reduce_fusion
  137.8 1.5 multiply_convert_fusion
  139.3 14.3 %all-gather = bf16[1,16,3584]{2,0,1:T(2,128)(2,1)S(1)} all-gather(bf16[1,4,3584]{2,0,1:T(2,128)(2,1)S(1)} %copy.48), channel_id=2, replica_groups=mesh['groups'=2,'ep'=4,'tp'=4] {'tp'}, dimensions={1}, use_global_device_ids=true | all-gather | bytes 143360 | tf_op jit(solution)/shard_map/all_gather | solution.py:79
  153.7 1.2 convolution_convert_fusion.1
  154.8 3.5 %all-to-all-start.1 = ((bf16[4,12,3584]{2,1,0:T(8,128)(2,1)}), bf16[4,12,3584]{2,1,0:T(8,128)(2,1)S(1)}, u32[]{:S(2)}, u32[]{:S(2)}) async-start(bf16[4,12,3584]{2,1,0:T(8,128)(2,1)} %convolution_convert_fusion.1), calls=%async_computation.1 | async-start | bytes 917504 | tf_op jit(solution)/shard_map/all_to_all | solution.py:100
  158.5 7.9 %all-to-all-done.1 = bf16[4,12,3584]{2,1,0:T(8,128)(2,1)S(1)} async-done(((bf16[4,12,3584]{2,1,0:T(8,128)(2,1)}), bf16[4,12,3584]{2,1,0:T(8,128)(2,1)S(1)}, u32[]{:S(2)}, u32[]{:S(2)}) %all-to-all-start.1) | async-done | bytes 344096 | tf_op jit(solution)/shard_map/all_to_all | solution.py:100
  166.4 2.8 %fusion.9 = f32[4,12,512]{2,1,0:T(8,128)S(1)} fusion(bf16[4,12,3584]{2,1,0:T(8,128)(2,1)S(1)} %all-to-all-done.1, bf16[1,2,3584,512]{3,2,1,0:T(8,128)(2,1)} %param.24), kind=kOutput, calls=%fused_computation.14 | convolution fusion | flops 176160768 | bytes 4112384 | tf_op jit(solution)/shard_map/scd,df->scf/dot_general | solution.py:101
  169.2 5.4 %convolution_convert_fusion = bf16[4,12,3584]{2,1,0:T(8,128)(2,1)} fusion(bf16[1,512,3584]{2,1,0:T(8,128)(2,1)} %param.25, bf16[4,12,3584]{2,1,0:T(8,128)(2,1)S(1)} %all-to-all-done.1, bf16[1,2,3584,512]{3,2,1,0:T(8,128)(2,1)} %param.24, f32[4,12,512]{2,1,0:T(8,128)S(1)} %fusion.9), kind=kOutput, calls=%fused_computation.3 | convolution fusion | flops 352641024 | bytes 8126464 | tf_op jit(solution)/shard_map/scf,fd->scd/dot_general | solution.py:108
  174.6 3.5 %all-to-all-start.2 = ((bf16[4,12,3584]{2,1,0:T(8,128)(2,1)}), bf16[4,12,3584]{2,1,0:T(8,128)(2,1)S(1)}, u32[]{:S(2)}, u32[]{:S(2)}) async-start(bf16[4,12,3584]{2,1,0:T(8,128)(2,1)} %convolution_convert_fusion), calls=%async_computation.2 | async-start | bytes 917504 | tf_op jit(solution)/shard_map/all_to_all | solution.py:111
  178.1 1.8 fusion.22
  180.0 6.2 %all-to-all-done.2 = bf16[4,12,3584]{2,1,0:T(8,128)(2,1)S(1)} async-done(((bf16[4,12,3584]{2,1,0:T(8,128)(2,1)}), bf16[4,12,3584]{2,1,0:T(8,128)(2,1)S(1)}, u32[]{:S(2)}, u32[]{:S(2)}) %all-to-all-start.2) | async-done | bytes 344096 | tf_op jit(solution)/shard_map/all_to_all | solution.py:111
  186.1 0.7 convolution_bitcast_fusion
  186.8 3.9 %fusion.5 = bf16[16,3584]{1,0:T(8,128)(2,1)} fusion(f32[16,3584]{1,0:T(8,128)S(1)} %convolution_bitcast_fusion, bf16[256,3584]{1,0:T(8,128)(2,1)} %param.27, bf16[2,3584,256]{2,1,0:T(8,128)(2,1)} %param.26, bf16[1,16,3584]{2,1,0:T(8,128)(2,1)S(1)} %copy.54, f32[16,256]{1,0:T(8,128)S(1)} %fusion.22), kind=kOutput, calls=%fused_computation.7 | convolution fusion | flops 58859520 | bytes 4145152 | tf_op jit(solution)/shard_map/dot_general | solution.py:125
  191.9 33.3 %all-reduce.7.cloned.1.call-done = bf16[16,3584]{1,0:T(8,128)(2,1)} async-done(((bf16[16,3584]{1,0:T(8,128)(2,1)}), bf16[16,3584]{1,0:T(8,128)(2,1)}) %all-reduce.7.cloned.1.call-update) | async-done | bytes 114704
  225.2 2.1 fusion.70
  (45 shorter events, 2.3 us)
Async XLA Ops:
  6.5 1.7 copy-start
  6.5 4.8 %copy-start.1 = (bf16[1,4,128,576]{2,3,1,0:T(8,128)(2,1)S(1)}, bf16[1,4,128,576]{2,3,1,0:T(8,128)(2,1)}, u32[]{:S(2)}) copy-start(bf16[1,4,128,576]{2,3,1,0:T(8,128)(2,1)} %param.15) | copy-start | bytes 1769476
  6.5 4.8 %copy-start.3 = (bf16[1,4,576]{2,1,0:T(4,128)(2,1)S(1)}, bf16[1,4,576]{2,1,0:T(4,128)(2,1)}, u32[]{:S(2)}) copy-start(bf16[1,4,576]{2,1,0:T(4,128)(2,1)} %param.17) | copy-start | bytes 13828
  6.5 129.7 %all-reduce.5.cloned.1.call-start = ((), (), s32[]{:S(2)}) async-start(), calls=%async_computation.3 | async-start | bytes 1835008
  38.0 6.9 %copy-start.4 = (bf16[3584]{0:T(1024)(128)(2,1)S(1)}, bf16[3584]{0:T(1024)(128)(2,1)}, u32[]{:S(2)}) copy-start(bf16[3584]{0:T(1024)(128)(2,1)} %param.22) | copy-start | bytes 21508
  38.0 7.0 %copy-start.5 = (s32[4,4,2]{1,2,0:T(2,128)S(1)}, s32[4,4,2]{1,2,0:T(2,128)}, u32[]{:S(2)}) copy-start(s32[4,4,2]{1,2,0:T(2,128)} %param.19) | copy-start | bytes 388
  38.0 7.3 %copy-start.8 = (u32[32]{0:T(128)S(1)}, u32[32]{0:T(128)}, u32[]{:S(2)}) copy-start(u32[32]{0:T(128)} %constant.40) | copy-start | bytes 388
  38.0 98.3 %copy-start.2 = (bf16[1,4,3584]{2,1,0:T(4,128)(2,1)S(1)}, bf16[1,4,3584]{2,1,0:T(4,128)(2,1)}, u32[]{:S(2)}) copy-start(bf16[1,4,3584]{2,1,0:T(4,128)(2,1)} %param.14) | copy-start | bytes 86020
  43.3 115.0 %copy-start.6 = (bf16[3584,4]{0,1:T(4,128)(2,1)S(1)}, bf16[3584,4]{0,1:T(4,128)(2,1)}, u32[]{:S(2)}) copy-start(bf16[3584,4]{0,1:T(4,128)(2,1)} %param.23) | copy-start | bytes 86020
  154.8 11.6 %all-to-all-start.1 = ((bf16[4,12,3584]{2,1,0:T(8,128)(2,1)}), bf16[4,12,3584]{2,1,0:T(8,128)(2,1)S(1)}, u32[]{:S(2)}, u32[]{:S(2)}) async-start(bf16[4,12,3584]{2,1,0:T(8,128)(2,1)} %convolution_convert_fusion.1), calls=%async_computation.1 | async-start | bytes 917504 | tf_op jit(solution)/shard_map/all_to_all | solution.py:100
  174.6 11.6 %all-to-all-start.2 = ((bf16[4,12,3584]{2,1,0:T(8,128)(2,1)}), bf16[4,12,3584]{2,1,0:T(8,128)(2,1)S(1)}, u32[]{:S(2)}, u32[]{:S(2)}) async-start(bf16[4,12,3584]{2,1,0:T(8,128)(2,1)} %convolution_convert_fusion), calls=%async_computation.2 | async-start | bytes 917504 | tf_op jit(solution)/shard_map/all_to_all | solution.py:111
  178.0 12.7 %copy-start.7 = (u32[32]{0:T(128)S(1)}, u32[32]{0:T(128)}, u32[]{:S(2)}) copy-start(u32[32]{0:T(128)} %constant.44) | copy-start | bytes 388
  178.1 47.2 %all-reduce.7.cloned.1.call-start = ((), (), s32[]{:S(2)}) async-start(), calls=%async_computation.4 | async-start | bytes 229376
Sparse Core Ops, SparseCore 0:
  45.0 91.1 all-reduce.4
  190.8 34.3 all-reduce.6
where the time goes:
time: 235 us; the launch traced here: 234 us
  waiting for transfers between devices  138 us (59%)
  blocking collectives  37.2 us (16%)
  matrix products  26.6 us (11%)
  between operations  15.1 us (6%)
  starting transfers between devices  6.97 us (3%)
  other arithmetic  6.16 us (3%)
  local copies, waits for them, and re-layouts  4.37 us (2%)
    unnamed x4, waiting for transfers between devices  124 us
    all_to_all x1, blocking collectives, on_device(): lax.all_to_all(latent_out, ('ep', 'tp'), split_axis=2, concat_axis=0, til...  22.8 us
    all_gather x1, blocking collectives, on_device(): lax.all_gather(normed.reshape(rows_here * steps_here, model_width), 'tp',...  14.3 us
    all_to_all x1, waiting for transfers between devices, on_device(): lax.all_to_all(outgoing, 'ep', split_axis=0, concat_axis=0, tiled=True)  7.89 us
    all_to_all x1, waiting for transfers between devices, on_device(): lax.all_to_all(produced.astype(jnp.bfloat16), 'ep', split_axis=0, concat_...  6.17 us
    dot_general x1, matrix products, on_device(): jnp.einsum('scf,fd->scd', activated, expert_out[0], preferred_element_typ...  5.4 us
    dot_general x1, matrix products, on_device(): jnp.einsum('rshv,hvd->rsd', head_vals, out_proj, preferred_element_type=j...  5.31 us
  transfers between devices with their start and end apart: 4, of which 4 were waited for; matrix products, arithmetic and copies ran while one was open for 2% of the time, Pallas kernels for 0%

commit v1 on v0

--- a/solution.py
+++ b/solution.py
@@ -61,7 +61,10 @@
     steps_here = hidden_in.shape[1]
     model_width = hidden_in.shape[2]
     latent_out = attend_block(queries, kv_cache, new_kv, lengths)
-    by_head = lax.all_to_all(latent_out, ("ep", "tp"), split_axis=2, concat_axis=0, tiled=True)
+    n_dev = lax.axis_size(("ep", "tp"))
+    blocks = jnp.stack(jnp.split(latent_out, n_dev, axis=2), axis=0)
+    blocks = lax.all_to_all(blocks, ("ep", "tp"), split_axis=0, concat_axis=0)
+    by_head = jnp.concatenate(blocks, axis=0)
     head_vals = jnp.einsum(
         "rshl,hlv->rshv", by_head, value_up, preferred_element_type=jnp.float32
     ).astype(jnp.bfloat16)

time: 235 us -> 281 us (1.20)
  local copies, waits for them, and re-layouts: 4.37 us -> 48.6 us
    another operation x0 -> x18, local copies, waits for them, and re-layouts: none -> 28 us  [on_device(): blocks = jnp.stack(jnp.split(latent_out, n_dev, axis=2), axis=0)]
    unnamed x22 -> x37, local copies, waits for them, and re-layouts: 2.08 us -> 18.7 us
  transfers between devices with their start and end apart: 4 -> 4, of which waited for: 4 -> 4; matrix products, arithmetic and copies ran while one was open for 2% -> 1% of each run, Pallas kernels for 0% -> 0%
where the time goes in v1:
time: 281 us; the launch traced here: 279 us
  waiting for transfers between devices  138 us (49%)
  local copies, waits for them, and re-layouts  48.6 us (17%)
  blocking collectives  37.4 us (13%)
  matrix products  26.9 us (10%)
  between operations  15.1 us (5%)
  starting transfers between devices  7.15 us (3%)
  other arithmetic  6.16 us (2%)
    unnamed x4, waiting for transfers between devices  124 us
    another operation x18, local copies, waits for them, and re-layouts, on_device(): blocks = jnp.stack(jnp.split(latent_out, n_dev, axis=2), axis=0)  28 us
    all_to_all x1, blocking collectives, on_device(): blocks = lax.all_to_all(blocks, ('ep', 'tp'), split_axis=0, concat_axis=0)  23 us
    unnamed x37, local copies, waits for them, and re-layouts  18.7 us
    all_gather x1, blocking collectives, on_device(): lax.all_gather(normed.reshape(rows_here * steps_here, model_width), 'tp',...  14.3 us
    all_to_all x1, waiting for transfers between devices, on_device(): lax.all_to_all(outgoing, 'ep', split_axis=0, concat_axis=0, tiled=True)  7.71 us
    all_to_all x1, waiting for transfers between devices, on_device(): lax.all_to_all(produced.astype(jnp.bfloat16), 'ep', split_axis=0, concat_...  6.17 us
  transfers between devices with their start and end apart: 4, of which 4 were waited for; matrix products, arithmetic and copies ran while one was open for 1% of the time, Pallas kernels for 0%

profile of v1, /device:TPU:0, one launch (start us, length us, event | category | flops | bytes accessed | tf_op | source)
XLA Modules:
  0.0 278.8 jit_solution(7044764936408304026)
XLA Ops:
  8.2 3.2 %fusion.6 = (f32[4,128]{1,0:T(4,128)S(1)}, f32[4,128,2048]{2,1,0:T(8,128)S(1)}) fusion(pred[2048]{0:T(1024)(128)(4,1)S(1)} %iota_compare_fusion.1, bf16[1,2048,576]{1,2,0:T(8,128)(2,1)S(1)} %copy-done, bf16[1,4,128,576]{2,3,1,0:T(8,128)(2,1)} %param.15), kind=kOutput, calls=%fused_computation.11 | convolution fusion | flops 1211104768 | bytes 7147520 | tf_op jit(solution)/shard_map/rshk,rck->rshc/dot_general | solution.py:16
  14.7 4.0 %slice_bitcast_fusion = (bf16[1,1,4,8,512]{3,4,2,1,0:T(8,128)(2,1)S(1)}, bf16[1,1,4,8,512]{3,4,2,1,0:T(8,128)(2,1)S(1)}, bf16[1,1,4,8,512]{3,4,2,1,0:T(8,128)(2,...) fusion(bf16[1,4,128,576]{2,3,1,0:T(8,128)(2,1)S(1)} %fusion.27), kind=kLoop, calls=%fused_computation.50 | loop fusion | bytes 1048576 | tf_op jit(solution)/shard_map/stack | solution.py:65
  20.5 1.8 copy.55
  24.2 1.8 copy.57
  26.0 1.8 copy.58
  27.8 1.8 copy.59
  31.4 1.8 copy.61
  33.2 1.8 copy.62
  35.0 1.8 copy.63
  36.9 1.8 copy.64
  59.3 23.0 %all_to_all.15 = bf16[16,1,4,8,512]{4,3,2,1,0:T(8,128)(2,1)} all-to-all(bf16[16,1,4,8,512]{4,3,2,1,0:T(8,128)(2,1)} %constant_dynamic-update-slice_fusion), channel_id=1, replica_groups=mesh['groups'=2,'ep'=4,'tp'=4] {'ep','tp'}, dimensions={0} | all-to-all | bytes 1048576 | tf_op jit(solution)/shard_map/all_to_all | solution.py:66
  82.4 5.6 %fusion.2 = f32[16,4,3584]{2,0,1:T(8,128)S(1)} fusion(bf16[8,128,3584]{2,1,0:T(8,128)(2,1)} %param.21, bf16[8,512,128]{2,1,0:T(8,128)(2,1)} %param.20, bf16[16,1,4,8,512]{4,3,2,1,0:T(8,128)(2,1)} %all_to_all.15), kind=kOutput, calls=%fused_computation.2 | convolution fusion | flops 536936448 | bytes 9830400 | tf_op jit(solution)/shard_map/rshv,hvd->rsd/dot_general | solution.py:72
  90.6 90.4 %all-reduce.5.cloned.1.call-done = f32[16,4,3584]{2,1,0:T(4,128)} async-done(((f32[16,4,3584]{2,1,0:T(4,128)}), f32[16,4,3584]{2,1,0:T(4,128)}) %all-reduce.5.cloned.1.call-update) | async-done | bytes 917520
  184.0 14.3 %all-gather = bf16[1,16,3584]{2,0,1:T(2,128)(2,1)S(1)} all-gather(bf16[1,4,3584]{2,0,1:T(2,128)(2,1)S(1)} %copy.76), channel_id=2, replica_groups=mesh['groups'=2,'ep'=4,'tp'=4] {'tp'}, dimensions={1}, use_global_device_ids=true | all-gather | bytes 143360 | tf_op jit(solution)/shard_map/all_gather | solution.py:82
  199.5 3.6 %all-to-all-start.1 = ((bf16[4,12,3584]{2,1,0:T(8,128)(2,1)}), bf16[4,12,3584]{2,1,0:T(8,128)(2,1)S(1)}, u32[]{:S(2)}, u32[]{:S(2)}) async-start(bf16[4,12,3584]{2,1,0:T(8,128)(2,1)} %convolution_convert_fusion.1), calls=%async_computation.1 | async-start | bytes 917504 | tf_op jit(solution)/shard_map/all_to_all | solution.py:103
  203.4 7.7 %all-to-all-done.1 = bf16[4,12,3584]{2,1,0:T(8,128)(2,1)S(1)} async-done(((bf16[4,12,3584]{2,1,0:T(8,128)(2,1)}), bf16[4,12,3584]{2,1,0:T(8,128)(2,1)S(1)}, u32[]{:S(2)}, u32[]{:S(2)}) %all-to-all-start.1) | async-done | bytes 344096 | tf_op jit(solution)/shard_map/all_to_all | solution.py:103
  211.1 2.8 fusion.9
  213.9 5.4 %convolution_convert_fusion = bf16[4,12,3584]{2,1,0:T(8,128)(2,1)} fusion(bf16[1,512,3584]{2,1,0:T(8,128)(2,1)} %param.25, bf16[4,12,3584]{2,1,0:T(8,128)(2,1)S(1)} %all-to-all-done.1, bf16[1,2,3584,512]{3,2,1,0:T(8,128)(2,1)} %param.24, f32[4,12,512]{2,1,0:T(8,128)S(1)} %fusion.9), kind=kOutput, calls=%fused_computation.3 | convolution fusion | flops 352641024 | bytes 8126464 | tf_op jit(solution)/shard_map/scf,fd->scd/dot_general | solution.py:111
  219.3 3.5 %all-to-all-start.2 = ((bf16[4,12,3584]{2,1,0:T(8,128)(2,1)}), bf16[4,12,3584]{2,1,0:T(8,128)(2,1)S(1)}, u32[]{:S(2)}, u32[]{:S(2)}) async-start(bf16[4,12,3584]{2,1,0:T(8,128)(2,1)} %convolution_convert_fusion), calls=%async_computation.2 | async-start | bytes 917504 | tf_op jit(solution)/shard_map/all_to_all | solution.py:114
  222.8 1.8 fusion.22
  224.6 6.2 %all-to-all-done.2 = bf16[4,12,3584]{2,1,0:T(8,128)(2,1)S(1)} async-done(((bf16[4,12,3584]{2,1,0:T(8,128)(2,1)}), bf16[4,12,3584]{2,1,0:T(8,128)(2,1)S(1)}, u32[]{:S(2)}, u32[]{:S(2)}) %all-to-all-start.2) | async-done | bytes 344096 | tf_op jit(solution)/shard_map/all_to_all | solution.py:114
  231.5 3.9 %fusion.5 = bf16[16,3584]{1,0:T(8,128)(2,1)} fusion(f32[16,3584]{1,0:T(8,128)S(1)} %convolution_bitcast_fusion, bf16[256,3584]{1,0:T(8,128)(2,1)} %param.27, bf16[2,3584,256]{2,1,0:T(8,128)(2,1)} %param.26, bf16[1,16,3584]{2,1,0:T(8,128)(2,1)S(1)} %copy.81, f32[16,256]{1,0:T(8,128)S(1)} %fusion.22), kind=kOutput, calls=%fused_computation.7 | convolution fusion | flops 58859520 | bytes 4145152 | tf_op jit(solution)/shard_map/dot_general | solution.py:128
  236.6 33.3 %all-reduce.7.cloned.1.call-done = bf16[16,3584]{1,0:T(8,128)(2,1)} async-done(((bf16[16,3584]{1,0:T(8,128)(2,1)}), bf16[16,3584]{1,0:T(8,128)(2,1)}) %all-reduce.7.cloned.1.call-update) | async-done | bytes 114704
  269.9 2.1 fusion.69
  (76 shorter events, 38.5 us)
Async XLA Ops:
  6.5 1.7 copy-start
  6.5 4.8 %copy-start.1 = (bf16[1,4,128,576]{2,3,1,0:T(8,128)(2,1)S(1)}, bf16[1,4,128,576]{2,3,1,0:T(8,128)(2,1)}, u32[]{:S(2)}) copy-start(bf16[1,4,128,576]{2,3,1,0:T(8,128)(2,1)} %param.15) | copy-start | bytes 1769476
  6.5 4.8 %copy-start.3 = (bf16[1,4,576]{2,1,0:T(4,128)(2,1)S(1)}, bf16[1,4,576]{2,1,0:T(4,128)(2,1)}, u32[]{:S(2)}) copy-start(bf16[1,4,576]{2,1,0:T(4,128)(2,1)} %param.17) | copy-start | bytes 13828
  6.5 174.4 %all-reduce.5.cloned.1.call-start = ((), (), s32[]{:S(2)}) async-start(), calls=%async_computation.3 | async-start | bytes 1835008
  82.4 7.2 %copy-start.4 = (bf16[3584]{0:T(1024)(128)(2,1)S(1)}, bf16[3584]{0:T(1024)(128)(2,1)}, u32[]{:S(2)}) copy-start(bf16[3584]{0:T(1024)(128)(2,1)} %param.22) | copy-start | bytes 21508
  82.4 7.2 %copy-start.5 = (s32[4,4,2]{1,2,0:T(2,128)S(1)}, s32[4,4,2]{1,2,0:T(2,128)}, u32[]{:S(2)}) copy-start(s32[4,4,2]{1,2,0:T(2,128)} %param.19) | copy-start | bytes 388
  82.4 7.6 %copy-start.8 = (u32[32]{0:T(128)S(1)}, u32[32]{0:T(128)}, u32[]{:S(2)}) copy-start(u32[32]{0:T(128)} %constant.40) | copy-start | bytes 388
  82.4 98.5 %copy-start.2 = (bf16[1,4,3584]{2,1,0:T(4,128)(2,1)S(1)}, bf16[1,4,3584]{2,1,0:T(4,128)(2,1)}, u32[]{:S(2)}) copy-start(bf16[1,4,3584]{2,1,0:T(4,128)(2,1)} %param.14) | copy-start | bytes 86020
  88.0 115.2 %copy-start.6 = (bf16[3584,4]{0,1:T(4,128)(2,1)S(1)}, bf16[3584,4]{0,1:T(4,128)(2,1)}, u32[]{:S(2)}) copy-start(bf16[3584,4]{0,1:T(4,128)(2,1)} %param.23) | copy-start | bytes 86020
  199.5 11.6 %all-to-all-start.1 = ((bf16[4,12,3584]{2,1,0:T(8,128)(2,1)}), bf16[4,12,3584]{2,1,0:T(8,128)(2,1)S(1)}, u32[]{:S(2)}, u32[]{:S(2)}) async-start(bf16[4,12,3584]{2,1,0:T(8,128)(2,1)} %convolution_convert_fusion.1), calls=%async_computation.1 | async-start | bytes 917504 | tf_op jit(solution)/shard_map/all_to_all | solution.py:103
  219.3 11.6 %all-to-all-start.2 = ((bf16[4,12,3584]{2,1,0:T(8,128)(2,1)}), bf16[4,12,3584]{2,1,0:T(8,128)(2,1)S(1)}, u32[]{:S(2)}, u32[]{:S(2)}) async-start(bf16[4,12,3584]{2,1,0:T(8,128)(2,1)} %convolution_convert_fusion), calls=%async_computation.2 | async-start | bytes 917504 | tf_op jit(solution)/shard_map/all_to_all | solution.py:114
  222.7 12.7 %copy-start.7 = (u32[32]{0:T(128)S(1)}, u32[32]{0:T(128)}, u32[]{:S(2)}) copy-start(u32[32]{0:T(128)} %constant.44) | copy-start | bytes 388
  222.8 47.1 %all-reduce.7.cloned.1.call-start = ((), (), s32[]{:S(2)}) async-start(), calls=%async_computation.4 | async-start | bytes 229376
Sparse Core Ops, SparseCore 0:
  89.7 91.1 all-reduce.4
  235.5 34.3 all-reduce.6
